TPU v7x, 32 devices: a whole 2x2x4 slice. The times are simulated.
32 devices in a mesh: dp: 8 (over z, y), tensor: 4 (over x, core).
Axes of the slice: x: 2, y: 2, z: 4, core: 2. Of those that a mesh axis runs over, the one named last changes fastest.
Arguments:
- grads: bfloat16 [8, 2, 4096, 1024], P('dp', None, None, 'tensor'), may hold values from -480 to 480
- master: float32 [2, 4096, 1024], P(None, 'dp', 'tensor'), may hold values from -0.09375 to 0.09375
- moment: float32 [2, 4096, 1024], P(None, 'dp', 'tensor'), may hold values from -0.06 to 0.06
- v_heads: float32 [8], P('tensor'), may hold values from 0.0001 to 0.001
- v_neurons: float32 [1024], P('tensor'), may hold values from 0.0001 to 0.001
Outputs:
- params: bfloat16 [2, 4096, 1024], P(None, None, 'tensor')
- new_master: float32 [2, 4096, 1024], P(None, 'dp', 'tensor')
- new_moment: float32 [2, 4096, 1024], P(None, 'dp', 'tensor')
- new_heads: float32 [8], P('tensor')
- new_neurons: float32 [1024], P('tensor')
All inputs are finite; a program needn't handle non-finite values.
Results may differ from a plain program's by a relative error of at most 0.001.
Values may be sent and summed in bfloat16 or wider, within the bound.
A program may use at most 64 MiB of HBM per device.

v0:
```python
import jax
import jax.numpy as jnp
from jax import lax
from jax.sharding import PartitionSpec as P

DIN = 4096
HEAD = 128
STEP = 2


def on_device(grads, master, moment, v_heads, v_neurons):
    replicas = lax.axis_size("dp")
    terms = grads[0].astype(jnp.float32)
    local_heads = v_heads.shape[0]
    summed = lax.psum_scatter(terms, "dp", scatter_dimension=1, tiled=True)
    gradient = summed / replicas
    key_rows = gradient[0].reshape(gradient.shape[1], local_heads, HEAD)
    heads_local = jnp.sum(key_rows * key_rows, axis=(0, 2))
    neurons_local = jnp.sum(gradient[1] * gradient[1], axis=0)
    head_sq, neuron_sq = lax.psum((heads_local, neurons_local), "dp")
    total = lax.psum(jnp.sum(head_sq) + jnp.sum(neuron_sq), "tensor")
    clip = jnp.minimum(1.0, 256.0 / (jnp.sqrt(total) + 1e-06))
    new_moment = 0.9 * moment + 0.1 * clip * gradient
    new_heads = 0.95 * v_heads + 0.05 * clip * clip * head_sq / (DIN * HEAD)
    new_neurons = 0.95 * v_neurons + 0.05 * clip * clip * neuron_sq / DIN
    second_fix = 1.0 - 0.95**STEP
    first_fix = 1.0 - 0.9**STEP
    key_denom = jnp.repeat(jnp.sqrt(new_heads / second_fix) + 1e-08, HEAD)
    value_denom = jnp.sqrt(new_neurons / second_fix) + 1e-08
    denom = jnp.stack([key_denom, value_denom])
    update = new_moment / first_fix / denom[:, None, :]
    new_master = master - 0.01 * (update + 0.1 * master)
    shard_params = new_master.astype(jnp.bfloat16)
    params = lax.all_gather(shard_params, "dp", axis=1, tiled=True)
    return (params, new_master, new_moment, new_heads, new_neurons)


def solution(mesh):
    in_specs = (
        P("dp", None, None, "tensor"),
        P(None, "dp", "tensor"),
        P(None, "dp", "tensor"),
        P("tensor"),
        P("tensor"),
    )
    out_specs = (
        P(None, None, "tensor"),
        P(None, "dp", "tensor"),
        P(None, "dp", "tensor"),
        P("tensor"),
        P("tensor"),
    )
    return jax.shard_map(
        on_device, mesh=mesh, in_specs=in_specs, out_specs=out_specs, check_vma=False
    )
```

profile of v0, /device:TPU:0, one launch (start us, length us, event | category | flops | bytes accessed | tf_op | source)
XLA Modules:
  0.0 280.1 jit_solution(5039654462741692976)
XLA Ops:
  7.2 0.0 reduce-scatter.2.cloned.1.call-start
  7.2 6.1 %bitcast_convert_fusion = f32[2,4096,256]{2,1,0:T(8,128)} fusion(bf16[1,2,4096,256]{3,2,1,0:T(8,128)(2,1)} %param.5), kind=kLoop, calls=%fused_computation | loop fusion | flops 2097152 | bytes 12582912 | tf_op jit(solution)/shard_map/convert_element_type | solution.py:13
  13.3 0.0 copy-start.3
  13.3 0.0 reduce-scatter.2.cloned.1.call-update
  13.3 0.0 all-gather.2.cloned.1.call-start
  13.4 150.3 %reduce-scatter.2.cloned.1.call-done = f32[2,512,256]{2,1,0:T(8,128)} async-done(((f32[2,4096,256]{2,1,0:T(8,128)}), f32[2,512,256]{2,1,0:T(8,128)}) %reduce-scatter.2.cloned.1.call-update) | async-done | bytes 1048592 | tf_op jit(solution)/shard_map/reduce_scatter | solution.py:15
  163.7 1.3 broadcast_multiply_fusion
  165.0 0.1 fusion
  165.1 0.1 bitcast_reduce_fusion
  165.2 19.5 %all-reduce = (f32[2]{0:T(128)S(1)}, f32[256]{0:T(256)S(1)}) all-reduce(f32[2]{0:T(128)S(1)} %bitcast_reduce_fusion, f32[256]{0:T(256)S(1)} %get-tuple-element.5), channel_id=1, replica_groups=mesh['dp'=8,'tensor'=4] {'dp'}, use_global_device_ids=true, to_apply=%region_3.0 | all-reduce | flops 258 | bytes 2064 | tf_op jit(solution)/shard_map/psum | solution.py:20
  184.7 0.6 reduce_sum.48
  185.3 0.6 reduce_sum.46
  187.2 6.2 %psum.23 = f32[]{:T(128)} all-reduce(f32[]{:T(128)S(6)} %add.35), channel_id=1, replica_groups=mesh['dp'=8,'tensor'=4] {'tensor'}, use_global_device_ids=true, to_apply=%region_8.9 | all-reduce | flops 1 | bytes 8 | tf_op jit(solution)/shard_map/psum | solution.py:21
  194.1 0.0 copy-done.3
  194.1 0.5 sqrt_add_fusion.1
  194.6 0.0 copy-done.2
  194.6 0.6 sqrt_add_fusion
  195.2 0.1 broadcast_in_dim.4
  195.2 0.0 copy-done
  195.2 0.0 copy-done.1
  195.3 3.0 %fusion.2 = (bf16[2,512,256]{2,1,0:T(8,128)(2,1)}, f32[2,512,256]{2,1,0:T(8,128)}, f32[2,512,256]{2,1,0:T(8,128)}) fusion(f32[2,512,256]{2,1,0:T(8,128)S(1)} %copy-done, f32[2,256]{1,0:T(2,128)S(1)} %pad_maximum_fusion, f32[2,512,256]{2,1,0:T(8,128)} %reduce-scatter.2.cloned.1.call-done, f32[]{:T(128)S(6)} %mul.68, f32[2,512,256]{2,1,0:T(8,128)S(1)} %copy-done.1), kind=kLoop, calls=%fused_computation.14 | loop fusion | flops 2621440 | bytes 5769220 | tf_op jit(solution)/shard_map/convert_element_type | solution.py:33
  198.3 0.0 all-gather.2.cloned.1.call-update
  198.3 70.4 %all-gather.2.cloned.1.call-done = bf16[2,4096,256]{2,1,0:T(8,128)(2,1)} async-done(((bf16[2,512,256]{2,1,0:T(8,128)(2,1)}), bf16[2,4096,256]{2,1,0:T(8,128)(2,1)}) %all-gather.2.cloned.1.call-update) | async-done | bytes 4194320 | tf_op jit(solution)/shard_map/all_gather | solution.py:34
  268.8 4.5 %copy.11 = bf16[2,4096,256]{2,1,0:T(8,128)(2,1)} copy(bf16[2,4096,256]{2,1,0:T(8,128)(2,1)} %all-gather.2.cloned.1.call-done) | data formatting | bytes 8388608
  (4 shorter events, 0.0 us)
Async XLA Ops:
  7.2 156.5 %reduce-scatter.2.cloned.1.call-start = ((), (), s32[]{:S(2)}) async-start(), calls=%async_computation.1 | async-start | bytes 9437184 | tf_op jit(solution)/shard_map/reduce_scatter | solution.py:15
  13.3 180.8 %copy-start.3 = (f32[2]{0:T(128)S(1)}, f32[2]{0:T(128)}, u32[]{:S(2)}) copy-start(f32[2]{0:T(128)} %param.8) | copy-start | bytes 28
  13.3 181.3 %copy-start.2 = (f32[256]{0:T(256)S(1)}, f32[256]{0:T(256)}, u32[]{:S(2)}) copy-start(f32[256]{0:T(256)} %param.9) | copy-start | bytes 3076
  13.3 182.0 %copy-start = (f32[2,512,256]{2,1,0:T(8,128)S(1)}, f32[2,512,256]{2,1,0:T(8,128)}, u32[]{:S(2)}) copy-start(f32[2,512,256]{2,1,0:T(8,128)} %param.6) | copy-start | bytes 3145732
  13.3 182.0 %copy-start.1 = (f32[2,512,256]{2,1,0:T(8,128)S(1)}, f32[2,512,256]{2,1,0:T(8,128)}, u32[]{:S(2)}) copy-start(f32[2,512,256]{2,1,0:T(8,128)} %param.7) | copy-start | bytes 3145732
  13.3 255.4 %all-gather.2.cloned.1.call-start = ((), (), s32[]{:S(2)}) async-start(), calls=%async_computation.2 | async-start | bytes 4718592 | tf_op jit(solution)/shard_map/all_gather | solution.py:34
Sparse Core Ops, SparseCore 0:
  13.4 150.1 reduce-scatter.1
  198.4 70.2 all-gather.1
where the time goes:
time: 280 us
  waiting for transfers between devices  221 us (79%)
  blocking collectives  25.6 us (9%)
  between operations  16.1 us (6%)
  other arithmetic  12.9 us (5%)
  local copies, waits for them, and re-layouts  4.55 us (2%)
    reduce_scatter x1, waiting for transfers between devices, on_device(): summed = lax.psum_scatter(terms, 'dp', scatter_dimension=1, tiled=True)  150 us
    all_gather x1, waiting for transfers between devices, on_device(): params = lax.all_gather(shard_params, 'dp', axis=1, tiled=True)  70.4 us
    psum x1, blocking collectives, on_device(): head_sq, neuron_sq = lax.psum((heads_local, neurons_local), 'dp')  19.5 us
    psum x1, blocking collectives, on_device(): total = lax.psum(jnp.sum(head_sq) + jnp.sum(neuron_sq), 'tensor')  6.17 us
    convert_element_type x1, other arithmetic, on_device(): terms = grads[0].astype(jnp.float32)  6.08 us
  transfers between devices with their start and end apart: 2, of which 2 were waited for; matrix products, arithmetic and copies ran while one was open for 0% of the time, Pallas kernels for 0%

commit v1 on v0

v1 whole, which is shorter than its diff:
```python
import functools

import jax
import jax.numpy as jnp
from jax import lax
from jax.experimental import pallas as pl
from jax.experimental.pallas import tpu as pltpu
from jax.sharding import PartitionSpec as P

HEAD = 128
STEP = 2
LIMIT = 480.0
MESH = pl.DeviceIdType.MESH
TILE = 32


def encode(x, scale):
    z = x * scale
    return (z * jnp.abs(z) * (z * z)).astype(jnp.bfloat16)


def decode(code, scale):
    y = code.astype(jnp.float32)
    root = lax.rsqrt(lax.rsqrt(jnp.abs(y))) * (1.0 / scale)
    return jnp.where(y < 0, -root, root)


def kernel(
    A, B, T, n_rows,
    grads, master, moment, v_heads, v_neurons,
    params, new_master, new_moment, new_v,
    own, raw, part_out, up_in, down_in, gsum, mas, mom, stat, stat_in, tot, tot_in,
    own_sem, mm_sem, raw_s, raw_r, part_s, up_r, down_r, stat_s, stat_r, tot_s, tot_r,
    zup_s, zup_r, zdn_s, zdn_r, in_s, in_r,
):
    nproj, n, R, C = grads.shape
    me = lax.axis_index("dp")
    mt = lax.axis_index("tensor")
    a, b = me // B, me % B
    tile = min(TILE, R)
    scale = 2.0**31 / (LIMIT * n)

    def at_dp(i):
        return {"dp": i}

    def peer(j):
        return (b + j) % B

    barrier = pltpu.get_barrier_semaphore()
    for j in range(1, n):
        pl.semaphore_signal(barrier, inc=1, device_id=at_dp((me + j) % n), device_id_type=MESH)
    for j in range(1, T):
        pl.semaphore_signal(barrier, inc=1, device_id={"tensor": (mt + j) % T}, device_id_type=MESH)

    def own_copy(at, p):
        return pltpu.make_async_copy(grads.at[p, at * B + b], own.at[at, p], own_sem.at[at, p])

    mm = [
        pltpu.make_async_copy(master, mas, mm_sem.at[0]),
        pltpu.make_async_copy(moment, mom, mm_sem.at[1]),
    ]

    def in_order(use):
        for d in range(A - 1, 0, -1):
            @pl.when(a + d <= A - 1)
            def _():
                use(a + d, 1)

            @pl.when(a - d >= 0)
            def _():
                use(a - d, -1)
        use(a, 0)

    def raw_copy(at, j, p):
        to = peer(j)
        return pltpu.make_async_remote_copy(
            src_ref=grads.at[p, at * B + to], dst_ref=raw.at[at, j - 1, p],
            send_sem=raw_s.at[at, j - 1, p], recv_sem=raw_r.at[at, j - 1, p],
            device_id=at_dp(a * B + to), device_id_type=MESH,
        )

    def start_own(at, side):
        for p in range(nproj):
            own_copy(at, p).start()

    def start_raw(at, side):
        for p in range(nproj):
            for j in range(1, B):
                raw_copy(at, j, p).start()

    in_order(start_own)
    for c in mm:
        c.start()
    pl.semaphore_wait(barrier, n - 1 + T - 1)
    in_order(start_raw)

    def up_copy(at, p):
        return pltpu.make_async_remote_copy(
            src_ref=part_out.at[at, p], dst_ref=up_in.at[at, p],
            send_sem=part_s.at[at, p], recv_sem=up_r.at[at, p],
            device_id=at_dp(jnp.minimum(me + B, n - 1)), device_id_type=MESH,
        )

    def down_copy(at, p):
        return pltpu.make_async_remote_copy(
            src_ref=part_out.at[at, p], dst_ref=down_in.at[at, p],
            send_sem=part_s.at[at, p], recv_sem=down_r.at[at, p],
            device_id=at_dp(jnp.maximum(me - B, 0)), device_id_type=MESH,
        )

    def local_sum(at, p, rows):
        x = own[at, p, rows].astype(jnp.float32)
        for j in range(B - 1):
            x = x + raw[at, j, p, rows].astype(jnp.float32)
        return x

    def tiles(body):
        def step(i, carry):
            body(pl.ds(pl.multiple_of(i * tile, tile), tile))
            return carry
        lax.fori_loop(0, R // tile, step, 0)

    def combine(at, side):
        for p in range(nproj):
            own_copy(at, p).wait()
            for j in range(1, B):
                raw_copy(at, j, p).wait_recv()
            if side == 0:
                tiles(lambda rows, p=p: gsum.__setitem__((p, rows), local_sum(at, p, rows)))
                for inn, copy, cond in ((up_in, up_copy, a > 0), (down_in, down_copy, a < A - 1)):
                    @pl.when(cond)
                    def _():
                        copy(at, p).wait_recv()

                        def add(rows):
                            gsum[p, rows] = gsum[p, rows] + decode(inn[at, p, rows], scale)
                        tiles(add)
                continue
            inn, copy = (up_in, up_copy) if side > 0 else (down_in, down_copy)
            first = (a == 0) if side > 0 else (a == A - 1)

            @pl.when(first)
            def _():
                def put(rows):
                    part_out[at, p, rows] = encode(local_sum(at, p, rows), scale)
                tiles(put)

            @pl.when(jnp.logical_not(first))
            def _():
                copy(at, p).wait_recv()

                def put(rows):
                    x = local_sum(at, p, rows) + decode(inn[at, p, rows], scale)
                    part_out[at, p, rows] = encode(x, scale)
                tiles(put)
            copy(at, p).start()

    in_order(combine)

    inv = 1.0 / n

    for p in range(nproj):
        def sq(i, acc):
            rows = pl.ds(pl.multiple_of(i * tile, tile), tile)
            g = gsum[p, rows] * inv
            gsum[p, rows] = g
            g = (g * g).reshape(tile // 8, 8, C)
            return acc + jnp.sum(g, axis=0)
        acc = lax.fori_loop(0, R // tile, sq, jnp.zeros((8, C), jnp.float32))
        stat[p : p + 1, :] = jnp.sum(acc, axis=0, keepdims=True)

    def stat_copy(j):
        return pltpu.make_async_remote_copy(
            src_ref=stat, dst_ref=stat_in.at[j - 1], send_sem=stat_s.at[j - 1], recv_sem=stat_r.at[j - 1],
            device_id=at_dp((me + j) % n), device_id_type=MESH,
        )

    for j in range(1, n):
        stat_copy(j).start()
    sums = stat[...]
    for j in range(1, n):
        stat_copy(j).wait_recv()
        sums = sums + stat_in[j - 1]
    tot[...] = jnp.broadcast_to(jnp.sum(sums), tot.shape)

    def tot_copy(j):
        return pltpu.make_async_remote_copy(
            src_ref=tot, dst_ref=tot_in.at[j - 1], send_sem=tot_s.at[j - 1], recv_sem=tot_r.at[j - 1],
            device_id={"tensor": (mt + j) % T}, device_id_type=MESH,
        )

    for j in range(1, T):
        tot_copy(j).start()
    total = tot[0:1, :]
    for j in range(1, T):
        tot_copy(j).wait_recv()
        total = total + tot_in[j - 1, 0:1, :]
    clip = jnp.minimum(1.0, 256.0 / (jnp.sqrt(total) + 1e-06))
    clip = jnp.concatenate([clip] * (C // HEAD), axis=1)
    heads = []
    for h in range(C // HEAD):
        head = jnp.sum(sums[0:1, h * HEAD : (h + 1) * HEAD], axis=1, keepdims=True)
        heads.append(0.95 * v_heads[h] + 0.05 * (clip * clip)[:, :HEAD] * head / (n_rows * HEAD))
    v_key = jnp.concatenate(heads, axis=1)
    v_val = 0.95 * v_neurons[...] + 0.05 * clip * clip * sums[1:2, :] / n_rows
    new_v[0:1, :] = v_key
    new_v[1:2, :] = v_val
    second_fix = 1.0 - 0.95**STEP
    first_fix = 1.0 - 0.9**STEP
    for c in mm:
        c.wait()

    def up_gather(at, p):
        return pltpu.make_async_remote_copy(
            src_ref=params.at[p, at * B + b], dst_ref=params.at[p, at * B + b],
            send_sem=zup_s.at[at, p], recv_sem=zup_r.at[at, p],
            device_id=at_dp(jnp.minimum(me + B, n - 1)), device_id_type=MESH,
        )

    def down_gather(at, p):
        return pltpu.make_async_remote_copy(
            src_ref=params.at[p, at * B + b], dst_ref=params.at[p, at * B + b],
            send_sem=zdn_s.at[at, p], recv_sem=zdn_r.at[at, p],
            device_id=at_dp(jnp.maximum(me - B, 0)), device_id_type=MESH,
        )

    def in_gather(at, j, p, col):
        return pltpu.make_async_remote_copy(
            src_ref=params.at[p, at * B + col], dst_ref=params.at[p, at * B + col],
            send_sem=in_s.at[at, j - 1, p], recv_sem=in_r.at[at, j - 1, p],
            device_id=at_dp(a * B + peer(j)), device_id_type=MESH,
        )

    for p in range(nproj):
        v = v_key if p == 0 else v_val
        rate = 1.0 / (first_fix * (jnp.sqrt(v / second_fix) + 1e-08))
        gain = 0.1 * clip

        def update(rows):
            fresh = 0.9 * mom[p, rows] + gain * gsum[p, rows]
            w = mas[p, rows]
            w = w - 0.01 * (fresh * rate + 0.1 * w)
            new_moment[p, rows] = fresh
            new_master[p, rows] = w
            params[p, me, rows] = w.astype(jnp.bfloat16)
        tiles(update)
        for j in range(1, B):
            in_gather(a, j, p, b).start()

        @pl.when(a < A - 1)
        def _():
            up_gather(a, p).start()

        @pl.when(a > 0)
        def _():
            down_gather(a, p).start()

    for d in range(1, A):
        for p in range(nproj):
            @pl.when(a - d >= 0)
            def _():
                at = a - d
                up_gather(at, p).wait_recv()

                @pl.when(a < A - 1)
                def _():
                    up_gather(at, p).start()
                for j in range(1, B):
                    in_gather(at, j, p, b).start()

            @pl.when(a + d <= A - 1)
            def _():
                at = a + d
                down_gather(at, p).wait_recv()

                @pl.when(a > 0)
                def _():
                    down_gather(at, p).start()
                for j in range(1, B):
                    in_gather(at, j, p, b).start()

    def finish(at, side):
        for p in range(nproj):
            for j in range(1, B):
                raw_copy(at, j, p).wait_send()
            if side > 0:
                up_copy(at, p).wait_send()
            elif side < 0:
                down_copy(at, p).wait_send()
            if side <= 0:
                @pl.when(a < A - 1)
                def _():
                    up_gather(at, p).wait_send()
            if side >= 0:
                @pl.when(a > 0)
                def _():
                    down_gather(at, p).wait_send()
            for j in range(1, B):
                in_gather(at, j, p, b).wait_send()
                in_gather(at, j, p, (b - j + B) % B).wait_recv()

    in_order(finish)
    for j in range(1, n):
        stat_copy(j).wait_send()
    for j in range(1, T):
        tot_copy(j).wait_send()


def inner_size(mesh):
    line = mesh.devices.reshape(mesh.shape["dp"], -1)[:, 0]
    n = len(line)
    spots = [getattr(d, "coords", None) for d in line]
    if any(s is None or len(s) < 3 for s in spots):
        return 2 if n % 2 == 0 else 1
    inner = sum(s[2] == spots[0][2] for s in spots)
    return inner if n % inner == 0 else 1


def on_device(B, grads, master, moment, v_heads, v_neurons):
    n, T = lax.axis_size("dp"), lax.axis_size("tensor")
    A = n // B
    _, nproj, rows, C = grads.shape
    R = rows // n
    f32, bf16 = jnp.float32, jnp.bfloat16
    dma = pltpu.SemaphoreType.DMA
    vmem = pl.BlockSpec(memory_space=pltpu.VMEM)
    hbm = pl.BlockSpec(memory_space=pl.ANY)
    block = (nproj, R, C)
    inner = max(B - 1, 1)
    params, new_master, new_moment, new_v = pl.pallas_call(
        functools.partial(kernel, A, B, T, rows),
        name="adam_mini",
        out_shape=[
            jax.ShapeDtypeStruct((nproj, n, R, C), bf16),
            jax.ShapeDtypeStruct(block, f32),
            jax.ShapeDtypeStruct(block, f32),
            jax.ShapeDtypeStruct((nproj, C), f32),
        ],
        in_specs=[hbm, hbm, hbm, pl.BlockSpec(memory_space=pltpu.SMEM), vmem],
        out_specs=[vmem] * 4,
        scratch_shapes=[
            pltpu.VMEM((A, *block), bf16),
            pltpu.VMEM((A, inner, *block), bf16),
            pltpu.VMEM((A, *block), bf16),
            pltpu.VMEM((A, *block), bf16),
            pltpu.VMEM((A, *block), bf16),
            pltpu.VMEM(block, f32),
            pltpu.VMEM(block, f32),
            pltpu.VMEM(block, f32),
            pltpu.VMEM((nproj, C), f32),
            pltpu.VMEM((n - 1, nproj, C), f32),
            pltpu.VMEM((8, HEAD), f32),
            pltpu.VMEM((T - 1, 8, HEAD), f32),
            dma((A, nproj)), dma((2,)),
            dma((A, inner, nproj)), dma((A, inner, nproj)),
            dma((A, nproj)), dma((A, nproj)), dma((A, nproj)),
            dma((n - 1,)), dma((n - 1,)), dma((T - 1,)), dma((T - 1,)),
            dma((A, nproj)), dma((A, nproj)), dma((A, nproj)), dma((A, nproj)),
            dma((A, inner, nproj)), dma((A, inner, nproj)),
        ],
        compiler_params=pltpu.CompilerParams(
            collective_id=0, has_side_effects=True, vmem_limit_bytes=48 * 2**20
        ),
    )(grads.reshape(nproj, n, R, C), master, moment, v_heads, v_neurons.reshape(1, C))
    new_heads = new_v[0].reshape(-1, HEAD)[:, 0]
    return (params.reshape(nproj, rows, C), new_master, new_moment, new_heads, new_v[1])


def solution(mesh):
    in_specs = (
        P("dp", None, None, "tensor"),
        P(None, "dp", "tensor"),
        P(None, "dp", "tensor"),
        P("tensor"),
        P("tensor"),
    )
    out_specs = (
        P(None, None, "tensor"),
        P(None, "dp", "tensor"),
        P(None, "dp", "tensor"),
        P("tensor"),
        P("tensor"),
    )
    return jax.shard_map(
        functools.partial(on_device, inner_size(mesh)),
        mesh=mesh, in_specs=in_specs, out_specs=out_specs, check_vma=False,
    )
```

time: 280 us -> 123 us (0.44)
  waiting for transfers between devices: 221 us -> 0 us
  Pallas kernels: 0 us -> 110 us
  blocking collectives: 25.6 us -> 0 us
  between operations: 16.1 us -> 0.65 us
  other arithmetic: 12.9 us -> 0 us
  local copies, waits for them, and re-layouts: 4.55 us -> 11.3 us
    reduce_scatter x1 -> x0, waiting for transfers between devices: 150 us -> none  [on_device(): summed = lax.psum_scatter(terms, 'dp', scatter_dimension=1, tiled=True)]
    pallas_call x0 -> x1, Pallas kernels: none -> 110 us  [on_device(): pl.pallas_call(functools.partial(kernel, A, B, T, rows), name='adam_mini'...]
    all_gather x1 -> x0, waiting for transfers between devices: 70.4 us -> none  [on_device(): params = lax.all_gather(shard_params, 'dp', axis=1, tiled=True)]
    psum x2 -> x0, blocking collectives: 25.6 us -> none  [the longest x1 19.5 us: on_device(): head_sq, neuron_sq = lax.psum((heads_local, neurons_local), 'dp')]
    convert_element_type x2 -> x0, other arithmetic: 9.12 us -> none  [the longest x1 6.08 us: on_device(): terms = grads[0].astype(jnp.float32)]
    unnamed x9 -> x12, local copies, waits for them, and re-layouts: 4.48 us -> 10.8 us
  transfers between devices with their start and end apart: 2 -> 0, of which waited for: 2 -> 0; matrix products, arithmetic and copies ran while one was open for 0% -> 0% of each run, Pallas kernels for 0% -> 0%
where the time goes in v1:
time: 123 us; the launch traced here: 122 us
  Pallas kernels  110 us (89%)
  local copies, waits for them, and re-layouts  11.3 us (9%)
    pallas_call x1, Pallas kernels, on_device(): pl.pallas_call(functools.partial(kernel, A, B, T, rows), name='adam_mini'...  110 us
    unnamed x12, local copies, waits for them, and re-layouts  10.8 us

profile of v1, /device:TPU:0, one launch (start us, length us, event | category | flops | bytes accessed | tf_op | source)
XLA Modules:
  0.0 122.4 jit_solution(1228421178019218222)
XLA Ops:
  0.6 0.0 copy-start
  0.6 1.2 copy-done
  1.9 0.0 copy-start.1
  1.9 1.2 copy-done.1
  3.1 0.0 copy-start.2
  3.1 0.7 copy-done.2
  3.8 0.0 copy-start.3
  3.8 0.7 copy-done.3
  4.4 110.4 %adam_mini.1 = (bf16[2,8,512,256]{3,2,1,0:T(8,128)(2,1)}, f32[2,512,256]{2,1,0:T(8,128)S(1)}, f32[2,512,256]{2,1,0:T(8,128)S(1)}, f32[2,256]{1,0:T(2,128)S(1)}) custom-call(bf16[2,8,512,256]{3,2,1,0:T(8,128)(2,1)} %bitcast.8, f32[2,512,256]{2,1,0:T(8,128)S(1)} %copy-done, f32[2,512,256]{2,1,0:T(8,128)S(1)} %copy-done.1, f32[2]{0:T(128)S(1)} %copy-done.3, ...), custom_call_target="tpu_custom_call" | custom-call | tf_op jit(solution)/shard_map/adam_mini/pallas_call | solution.py:330
  114.8 0.6 fusion
  115.4 0.6 copy.11
  116.0 4.5 %copy.15 = bf16[2,4096,256]{2,1,0:T(8,128)(2,1)} copy(bf16[2,4096,256]{2,1,0:T(8,128)(2,1)} %bitcast.9) | data formatting | bytes 8388608
  120.4 1.0 copy.16
  121.4 1.0 copy.17
Async XLA Ops:
  0.6 1.2 %copy-start = (f32[2,512,256]{2,1,0:T(8,128)S(1)}, f32[2,512,256]{2,1,0:T(8,128)}, u32[]{:S(2)}) copy-start(f32[2,512,256]{2,1,0:T(8,128)} %master.1) | copy-start | bytes 3145732
  1.9 1.2 %copy-start.1 = (f32[2,512,256]{2,1,0:T(8,128)S(1)}, f32[2,512,256]{2,1,0:T(8,128)}, u32[]{:S(2)}) copy-start(f32[2,512,256]{2,1,0:T(8,128)} %moment.1) | copy-start | bytes 3145732
  3.1 0.7 copy-start.2
  3.8 0.7 copy-start.3

commit v2 on v1

--- a/solution.py
+++ b/solution.py
@@ -12,6 +12,8 @@
 LIMIT = 480.0
 MESH = pl.DeviceIdType.MESH
 TILE = 32
+KERNEL_LIMIT = 40 * 2**20
+WRITER_LIMIT = 16 * 2**20
 
 
 def encode(x, scale):
@@ -29,9 +31,9 @@
     A, B, T, n_rows,
     grads, master, moment, v_heads, v_neurons,
     params, new_master, new_moment, new_v,
-    own, raw, part_out, up_in, down_in, gsum, mas, mom, stat, stat_in, tot, tot_in,
+    own, raw, xown, xin, xout, part_out, up_in, down_in, gsum, mas, mom, stat, stat_in, tot, tot_in,
     own_sem, mm_sem, raw_s, raw_r, part_s, up_r, down_r, stat_s, stat_r, tot_s, tot_r,
-    zup_s, zup_r, zdn_s, zdn_r, in_s, in_r,
+    zup_s, zup_r, zdn_s, zdn_r, in_s, in_r, xown_sem, xin_s, xin_r, xg_s, xg_r,
 ):
     nproj, n, R, C = grads.shape
     me = lax.axis_index("dp")
@@ -39,6 +41,16 @@
     a, b = me // B, me % B
     tile = min(TILE, R)
     scale = 2.0**31 / (LIMIT * n)
+    balanced = A >= 4 and B >= 2
+    last = nproj - 1
+    mated = jnp.logical_or(a <= 1, a >= A - 2) if balanced else jnp.bool_(False)
+    mate = jnp.where(a <= 1, 1 - a, 2 * A - 3 - a) if balanced else a
+
+    def unless_mate(at, p, use):
+        if balanced and p == last:
+            pl.when(jnp.logical_not(jnp.logical_and(mated, at == mate)))(use)
+        else:
+            use()
 
     def at_dp(i):
         return {"dp": i}
@@ -60,16 +72,18 @@
         pltpu.make_async_copy(moment, mom, mm_sem.at[1]),
     ]
 
-    def in_order(use):
+    def in_order(use, after=None):
         for d in range(A - 1, 0, -1):
             @pl.when(a + d <= A - 1)
             def _():
-                use(a + d, 1)
+                use(a + d, 1, d)
 
             @pl.when(a - d >= 0)
             def _():
-                use(a - d, -1)
-        use(a, 0)
+                use(a - d, -1, d)
+            if after is not None and d == A - 1:
+                after()
+        use(a, 0, 0)
 
     def raw_copy(at, j, p):
         to = peer(j)
@@ -79,19 +93,52 @@
             device_id=at_dp(a * B + to), device_id_type=MESH,
         )
 
-    def start_own(at, side):
+    def start_own(at, side, d):
         for p in range(nproj):
             own_copy(at, p).start()
 
-    def start_raw(at, side):
+    def start_raw(at, side, d):
         for p in range(nproj):
+            def go(p=p):
+                for j in range(1, B):
+                    raw_copy(at, j, p).start()
+            if balanced and p == last and d <= 1:
+                skip = mated if side == 0 else jnp.logical_and(mated, at == mate)
+                pl.when(jnp.logical_not(skip))(go)
+            else:
+                go()
+
+    def mate_raw(j):
+        return pltpu.make_async_remote_copy(
+            src_ref=grads.at[last, mate * B + peer(j)], dst_ref=xin.at[j - 1],
+            send_sem=xin_s.at[j - 1], recv_sem=xin_r.at[j - 1],
+            device_id=at_dp(mate * B + b), device_id_type=MESH,
+        )
+
+    def mate_own(j):
+        return pltpu.make_async_copy(grads.at[last, a * B + peer(j)], xown.at[j - 1], xown_sem.at[j - 1])
+
+    def mate_sum(j):
+        return pltpu.make_async_remote_copy(
+            src_ref=xout.at[j - 1], dst_ref=raw.at[a, j - 1, last],
+            send_sem=raw_s.at[a, j - 1, last], recv_sem=raw_r.at[a, j - 1, last],
+            device_id=at_dp(a * B + peer(j)), device_id_type=MESH,
+        )
+
+    in_order(start_own)
+    if balanced:
+        @pl.when(mated)
+        def _():
             for j in range(1, B):
-                raw_copy(at, j, p).start()
-
-    in_order(start_own)
+                mate_own(j).start()
     for c in mm:
         c.start()
     pl.semaphore_wait(barrier, n - 1 + T - 1)
+    if balanced:
+        @pl.when(mated)
+        def _():
+            for j in range(1, B):
+                mate_raw(j).start()
     in_order(start_raw)
 
     def up_copy(at, p):
@@ -108,11 +155,25 @@
             device_id=at_dp(jnp.maximum(me - B, 0)), device_id_type=MESH,
         )
 
-    def local_sum(at, p, rows):
+    def local_sum(at, p, rows, kind="raw"):
         x = own[at, p, rows].astype(jnp.float32)
-        for j in range(B - 1):
-            x = x + raw[at, j, p, rows].astype(jnp.float32)
+        for j in range(B - 1 if kind != "own" else 0):
+            y = raw[at, j, p, rows]
+            x = x + (decode(y, scale) if kind == "coded" else y.astype(jnp.float32))
         return x
+
+    def send_mate_sums():
+        @pl.when(mated)
+        def _():
+            for j in range(1, B):
+                mate_own(j).wait()
+                mate_raw(j).wait_recv()
+
+                def put(rows, j=j):
+                    x = xown[j - 1, rows].astype(jnp.float32) + xin[j - 1, rows].astype(jnp.float32)
+                    xout[j - 1, rows] = encode(x, scale)
+                tiles(put)
+                mate_sum(j).start()
 
     def tiles(body):
         def step(i, carry):
@@ -120,42 +181,53 @@
             return carry
         lax.fori_loop(0, R // tile, step, 0)
 
-    def combine(at, side):
+    def combine(at, side, d):
         for p in range(nproj):
-            own_copy(at, p).wait()
+            if balanced and p == last and d <= 1:
+                odd = mated if side == 0 else jnp.logical_and(mated, at == mate)
+                pl.when(odd)(functools.partial(combine_one, at, side, p, "coded" if side == 0 else "own"))
+                pl.when(jnp.logical_not(odd))(functools.partial(combine_one, at, side, p, "raw"))
+            else:
+                combine_one(at, side, p, "raw")
+
+    def combine_one(at, side, p, kind):
+        own_copy(at, p).wait()
+        if kind != "own":
             for j in range(1, B):
                 raw_copy(at, j, p).wait_recv()
-            if side == 0:
-                tiles(lambda rows, p=p: gsum.__setitem__((p, rows), local_sum(at, p, rows)))
-                for inn, copy, cond in ((up_in, up_copy, a > 0), (down_in, down_copy, a < A - 1)):
-                    @pl.when(cond)
-                    def _():
-                        copy(at, p).wait_recv()
-
-                        def add(rows):
-                            gsum[p, rows] = gsum[p, rows] + decode(inn[at, p, rows], scale)
-                        tiles(add)
-                continue
-            inn, copy = (up_in, up_copy) if side > 0 else (down_in, down_copy)
-            first = (a == 0) if side > 0 else (a == A - 1)
-
-            @pl.when(first)
-            def _():
-                def put(rows):
-                    part_out[at, p, rows] = encode(local_sum(at, p, rows), scale)
-                tiles(put)
-
-            @pl.when(jnp.logical_not(first))
-            def _():
-                copy(at, p).wait_recv()
-
-                def put(rows):
-                    x = local_sum(at, p, rows) + decode(inn[at, p, rows], scale)
-                    part_out[at, p, rows] = encode(x, scale)
-                tiles(put)
-            copy(at, p).start()
-
-    in_order(combine)
+        if side == 0:
+            def begin(rows):
+                gsum[p, rows] = local_sum(at, p, rows, kind)
+            tiles(begin)
+            for inn, copy, cond in ((up_in, up_copy, a > 0), (down_in, down_copy, a < A - 1)):
+                @pl.when(cond)
+                def _():
+                    copy(at, p).wait_recv()
+
+                    def add(rows):
+                        gsum[p, rows] = gsum[p, rows] + decode(inn[at, p, rows], scale)
+                    tiles(add)
+            return
+        inn, copy = (up_in, up_copy) if side > 0 else (down_in, down_copy)
+        first = (a == 0) if side > 0 else (a == A - 1)
+
+        @pl.when(first)
+        def _():
+            def put(rows):
+                part_out[at, p, rows] = encode(local_sum(at, p, rows, kind), scale)
+            tiles(put)
+
+        @pl.when(jnp.logical_not(first))
+        def _():
+            copy(at, p).wait_recv()
+
+            def put(rows):
+                x = local_sum(at, p, rows, kind) + decode(inn[at, p, rows], scale)
+                part_out[at, p, rows] = encode(x, scale)
+            tiles(put)
+        copy(at, p).start()
+
+    in_order(combine, send_mate_sums if balanced else None)
 
     inv = 1.0 / n
 
@@ -231,6 +303,16 @@
             device_id=at_dp(a * B + peer(j)), device_id_type=MESH,
         )
 
+    def column_from(j):
+        return (b - j + B) % B
+
+    def mate_gather(at, j):
+        block = params.at[last, at * B + column_from(j)]
+        return pltpu.make_async_remote_copy(
+            src_ref=block, dst_ref=block, send_sem=xg_s.at[j - 1], recv_sem=xg_r.at[j - 1],
+            device_id=at_dp(mate * B + b), device_id_type=MESH,
+        )
+
     for p in range(nproj):
         v = v_key if p == 0 else v_val
         rate = 1.0 / (first_fix * (jnp.sqrt(v / second_fix) + 1e-08))
@@ -265,8 +347,11 @@
                 @pl.when(a < A - 1)
                 def _():
                     up_gather(at, p).start()
-                for j in range(1, B):
-                    in_gather(at, j, p, b).start()
+
+                def across():
+                    for j in range(1, B):
+                        in_gather(at, j, p, b).start()
+                unless_mate(at, p, across)
 
             @pl.when(a + d <= A - 1)
             def _():
@@ -276,13 +361,37 @@
                 @pl.when(a > 0)
                 def _():
                     down_gather(at, p).start()
+
+                def across():
+                    for j in range(1, B):
+                        in_gather(at, j, p, b).start()
+                unless_mate(at, p, across)
+        if balanced and d == 2:
+            @pl.when(mated)
+            def _():
                 for j in range(1, B):
-                    in_gather(at, j, p, b).start()
-
-    def finish(at, side):
+                    in_gather(a, j, last, column_from(j)).wait_recv()
+                    mate_gather(a, j).start()
+
+    def finish(at, side, d):
         for p in range(nproj):
-            for j in range(1, B):
-                raw_copy(at, j, p).wait_send()
+            def across(p=p):
+                for j in range(1, B):
+                    raw_copy(at, j, p).wait_send()
+                    in_gather(at, j, p, b).wait_send()
+
+            def arrive(p=p):
+                for j in range(1, B):
+                    in_gather(at, j, p, column_from(j)).wait_recv()
+            if side == 0:
+                across()
+                if balanced and p == last:
+                    pl.when(jnp.logical_not(mated))(arrive)
+                else:
+                    arrive()
+            else:
+                unless_mate(at, p, across)
+                unless_mate(at, p, arrive)
             if side > 0:
                 up_copy(at, p).wait_send()
             elif side < 0:
@@ -295,15 +404,35 @@
                 @pl.when(a > 0)
                 def _():
                     down_gather(at, p).wait_send()
+
+    in_order(finish)
+    if balanced:
+        @pl.when(mated)
+        def _():
             for j in range(1, B):
-                in_gather(at, j, p, b).wait_send()
-                in_gather(at, j, p, (b - j + B) % B).wait_recv()
-
-    in_order(finish)
+                mate_raw(j).wait_send()
+                mate_gather(a, j).wait_send()
+                mate_gather(mate, j).wait_recv()
     for j in range(1, n):
         stat_copy(j).wait_send()
     for j in range(1, T):
         tot_copy(j).wait_send()
+
+
+def writer(params, new_master, new_moment, new_v, params_out, master_out, moment_out, heads, neurons, sem):
+    copies = [
+        pltpu.make_async_copy(src, dst, sem.at[i])
+        for i, (src, dst) in enumerate(
+            ((params, params_out), (new_master, master_out), (new_moment, moment_out))
+        )
+    ]
+    for c in copies:
+        c.start()
+    for h in range(heads.shape[0]):
+        heads[h] = jnp.max(new_v[0:1, h * HEAD : (h + 1) * HEAD])
+    neurons[...] = new_v[1:2, :]
+    for c in copies:
+        c.wait()
 
 
 def inner_size(mesh):
@@ -324,7 +453,7 @@
     f32, bf16 = jnp.float32, jnp.bfloat16
     dma = pltpu.SemaphoreType.DMA
     vmem = pl.BlockSpec(memory_space=pltpu.VMEM)
-    hbm = pl.BlockSpec(memory_space=pl.ANY)
+    hbm = pl.BlockSpec(memory_space=pltpu.HBM)
     block = (nproj, R, C)
     inner = max(B - 1, 1)
     params, new_master, new_moment, new_v = pl.pallas_call(
@@ -341,6 +470,9 @@
         scratch_shapes=[
             pltpu.VMEM((A, *block), bf16),
             pltpu.VMEM((A, inner, *block), bf16),
+            pltpu.VMEM((inner, R, C), bf16),
+            pltpu.VMEM((inner, R, C), bf16),
+            pltpu.VMEM((inner, R, C), bf16),
             pltpu.VMEM((A, *block), bf16),
             pltpu.VMEM((A, *block), bf16),
             pltpu.VMEM((A, *block), bf16),
@@ -357,13 +489,31 @@
             dma((n - 1,)), dma((n - 1,)), dma((T - 1,)), dma((T - 1,)),
             dma((A, nproj)), dma((A, nproj)), dma((A, nproj)), dma((A, nproj)),
             dma((A, inner, nproj)), dma((A, inner, nproj)),
+            dma((inner,)), dma((inner,)), dma((inner,)), dma((inner,)), dma((inner,)),
         ],
         compiler_params=pltpu.CompilerParams(
-            collective_id=0, has_side_effects=True, vmem_limit_bytes=48 * 2**20
+            collective_id=0, has_side_effects=True, vmem_limit_bytes=KERNEL_LIMIT
         ),
     )(grads.reshape(nproj, n, R, C), master, moment, v_heads, v_neurons.reshape(1, C))
-    new_heads = new_v[0].reshape(-1, HEAD)[:, 0]
-    return (params.reshape(nproj, rows, C), new_master, new_moment, new_heads, new_v[1])
+    heads = v_heads.shape[0]
+    params, new_master, new_moment, new_heads, new_neurons = pl.pallas_call(
+        writer,
+        name="write_out",
+        out_shape=[
+            jax.ShapeDtypeStruct((nproj, n, R, C), bf16),
+            jax.ShapeDtypeStruct(block, f32),
+            jax.ShapeDtypeStruct(block, f32),
+            jax.ShapeDtypeStruct((heads,), f32),
+            jax.ShapeDtypeStruct((1, C), f32),
+        ],
+        in_specs=[vmem] * 4,
+        out_specs=[pl.BlockSpec(memory_space=pltpu.HBM)] * 3 + [pl.BlockSpec(memory_space=pltpu.SMEM), vmem],
+        scratch_shapes=[dma((3,))],
+        compiler_params=pltpu.CompilerParams(vmem_limit_bytes=WRITER_LIMIT),
+    )(params, new_master, new_moment, new_v)
+    return (
+        params.reshape(nproj, rows, C), new_master, new_moment, new_heads, new_neurons.reshape(C),
+    )
 
 
 def solution(mesh):

time: 123 us -> 110 us (0.89)
  Pallas kernels: 110 us -> 103 us
  local copies, waits for them, and re-layouts: 11.3 us -> 5.96 us
    pallas_call x1, Pallas kernels: 110 us -> 99.6 us  [on_device(): pl.pallas_call(functools.partial(kernel, A, B, T, rows), name='adam_mini'...]
    unnamed x12 -> x10, local copies, waits for them, and re-layouts: 10.8 us -> 5.96 us
    pallas_call x0 -> x1, Pallas kernels: none -> 3.26 us  [on_device(): pl.pallas_call(writer, name='write_out', out_shape=[jax.ShapeDtypeStruct(...]
where the time goes in v2:
time: 110 us
  Pallas kernels  103 us (94%)
  local copies, waits for them, and re-layouts  5.96 us (5%)
    pallas_call x1, Pallas kernels, on_device(): pl.pallas_call(functools.partial(kernel, A, B, T, rows), name='adam_mini'...  99.6 us
    unnamed x10, local copies, waits for them, and re-layouts  5.96 us
    pallas_call x1, Pallas kernels, on_device(): pl.pallas_call(writer, name='write_out', out_shape=[jax.ShapeDtypeStruct(...  3.26 us

profile of v2, /device:TPU:0, one launch (start us, length us, event | category | flops | bytes accessed | tf_op | source)
XLA Modules:
  0.0 109.5 jit_solution(11988273152381747838)
XLA Ops:
  0.6 0.0 copy-start
  0.6 2.2 %copy-done = bf16[1,2,4096,256]{3,2,1,0:T(8,128)(2,1)S(1)} copy-done((bf16[1,2,4096,256]{3,2,1,0:T(8,128)(2,1)S(1)}, bf16[1,2,4096,256]{3,2,1,0:T(8,128)(2,1)}, u32[]{:S(2)}) %copy-start) | copy-done | bytes 4194328
  2.8 0.0 copy-start.1
  2.8 1.2 %copy-done.1 = f32[2,512,256]{2,1,0:T(8,128)S(1)} copy-done((f32[2,512,256]{2,1,0:T(8,128)S(1)}, f32[2,512,256]{2,1,0:T(8,128)}, u32[]{:S(2)}) %copy-start.1) | copy-done | bytes 1048600
  4.0 0.0 copy-start.2
  4.0 1.2 %copy-done.2 = f32[2,512,256]{2,1,0:T(8,128)S(1)} copy-done((f32[2,512,256]{2,1,0:T(8,128)S(1)}, f32[2,512,256]{2,1,0:T(8,128)}, u32[]{:S(2)}) %copy-start.2) | copy-done | bytes 1048600
  5.3 0.0 copy-start.3
  5.3 0.7 copy-done.3
  6.0 0.0 copy-start.4
  6.0 0.7 copy-done.4
  6.6 99.6 %adam_mini.1 = (bf16[2,8,512,256]{3,2,1,0:T(8,128)(2,1)S(1)}, f32[2,512,256]{2,1,0:T(8,128)S(1)}, f32[2,512,256]{2,1,0:T(8,128)S(1)}, f32[2,256]{1,0:T(2,128)S(1)}) custom-call(bf16[2,8,512,256]{3,2,1,0:T(8,128)(2,1)S(1)} %bitcast.4, f32[2,512,256]{2,1,0:T(8,128)S(1)} %copy-done.1, f32[2,512,256]{2,1,0:T(8,128)S(1)} %copy-done.2, f32[2]{0:T(128)S(1)} %copy-done.4, ...), custom_call_target="tpu_custom_call" | custom-call | tf_op jit(solution)/shard_map/adam_mini/pallas_call | solution.py:459
  106.3 3.3 %write_out.1 = (bf16[2,8,512,256]{3,2,1,0:T(8,128)(2,1)}, f32[2,512,256]{2,1,0:T(8,128)}, f32[2,512,256]{2,1,0:T(8,128)}, f32[2]{0:T(128)}, f32[1,256]{1,0:T(1,128)}) custom-call(bf16[2,8,512,256]{3,2,1,0:T(8,128)(2,1)S(1)} %get-tuple-element.14.params, f32[2,512,256]{2,1,0:T(8,128)S(1)} %get-tuple-element.15.new_master, ...), custom_call_target="tpu_custom_call" | custom-call | tf_op jit(solution)/shard_map/write_out/pallas_call | solution.py:499
Async XLA Ops:
  0.6 2.2 %copy-start = (bf16[1,2,4096,256]{3,2,1,0:T(8,128)(2,1)S(1)}, bf16[1,2,4096,256]{3,2,1,0:T(8,128)(2,1)}, u32[]{:S(2)}) copy-start(bf16[1,2,4096,256]{3,2,1,0:T(8,128)(2,1)} %param.5) | copy-start | bytes 12582916
  2.8 1.2 %copy-start.1 = (f32[2,512,256]{2,1,0:T(8,128)S(1)}, f32[2,512,256]{2,1,0:T(8,128)}, u32[]{:S(2)}) copy-start(f32[2,512,256]{2,1,0:T(8,128)} %master.1) | copy-start | bytes 3145732
  4.0 1.2 %copy-start.2 = (f32[2,512,256]{2,1,0:T(8,128)S(1)}, f32[2,512,256]{2,1,0:T(8,128)}, u32[]{:S(2)}) copy-start(f32[2,512,256]{2,1,0:T(8,128)} %moment.1) | copy-start | bytes 3145732
  5.3 0.7 copy-start.3
  6.0 0.7 copy-start.4

commit v3 on v2

--- a/solution.py
+++ b/solution.py
@@ -12,7 +12,7 @@
 LIMIT = 480.0
 MESH = pl.DeviceIdType.MESH
 TILE = 32
-KERNEL_LIMIT = 40 * 2**20
+KERNEL_LIMIT = 43 * 2**20
 WRITER_LIMIT = 16 * 2**20
 
 
@@ -33,7 +33,7 @@
     params, new_master, new_moment, new_v,
     own, raw, xown, xin, xout, part_out, up_in, down_in, gsum, mas, mom, stat, stat_in, tot, tot_in,
     own_sem, mm_sem, raw_s, raw_r, part_s, up_r, down_r, stat_s, stat_r, tot_s, tot_r,
-    zup_s, zup_r, zdn_s, zdn_r, in_s, in_r, xown_sem, xin_s, xin_r, xg_s, xg_r,
+    zup_s, zup_r, zdn_s, zdn_r, in_s, in_r, xown_sem, xin_s, xin_r, xup_s, xup_r, xdn_s, xdn_r,
 ):
     nproj, n, R, C = grads.shape
     me = lax.axis_index("dp")
@@ -196,17 +196,30 @@
             for j in range(1, B):
                 raw_copy(at, j, p).wait_recv()
         if side == 0:
-            def begin(rows):
-                gsum[p, rows] = local_sum(at, p, rows, kind)
-            tiles(begin)
-            for inn, copy, cond in ((up_in, up_copy, a > 0), (down_in, down_copy, a < A - 1)):
-                @pl.when(cond)
-                def _():
-                    copy(at, p).wait_recv()
-
-                    def add(rows):
-                        gsum[p, rows] = gsum[p, rows] + decode(inn[at, p, rows], scale)
-                    tiles(add)
+            def close(up, down):
+                for used, inn, copy in ((up, up_in, up_copy), (down, down_in, down_copy)):
+                    if used:
+                        copy(at, p).wait_recv()
+
+                def one(i, acc):
+                    rows = pl.ds(pl.multiple_of(i * tile, tile), tile)
+                    g = local_sum(at, p, rows, kind)
+                    if up:
+                        g = g + decode(up_in[at, p, rows], scale)
+                    if down:
+                        g = g + decode(down_in[at, p, rows], scale)
+                    g = g * (1.0 / n)
+                    gsum[p, rows] = g
+                    return acc + jnp.sum((g * g).reshape(tile // 8, 8, C), axis=0)
+                acc = lax.fori_loop(0, R // tile, one, jnp.zeros((8, C), jnp.float32))
+                stat[p : p + 1, :] = jnp.sum(acc, axis=0, keepdims=True)
+
+            if A == 1:
+                close(False, False)
+            else:
+                pl.when(a == 0)(lambda: close(False, True))
+                pl.when(a == A - 1)(lambda: close(True, False))
+                pl.when(jnp.logical_and(a > 0, a < A - 1))(lambda: close(True, True))
             return
         inn, copy = (up_in, up_copy) if side > 0 else (down_in, down_copy)
         first = (a == 0) if side > 0 else (a == A - 1)
@@ -228,18 +241,6 @@
         copy(at, p).start()
 
     in_order(combine, send_mate_sums if balanced else None)
-
-    inv = 1.0 / n
-
-    for p in range(nproj):
-        def sq(i, acc):
-            rows = pl.ds(pl.multiple_of(i * tile, tile), tile)
-            g = gsum[p, rows] * inv
-            gsum[p, rows] = g
-            g = (g * g).reshape(tile // 8, 8, C)
-            return acc + jnp.sum(g, axis=0)
-        acc = lax.fori_loop(0, R // tile, sq, jnp.zeros((8, C), jnp.float32))
-        stat[p : p + 1, :] = jnp.sum(acc, axis=0, keepdims=True)
 
     def stat_copy(j):
         return pltpu.make_async_remote_copy(
@@ -306,12 +307,25 @@
     def column_from(j):
         return (b - j + B) % B
 
-    def mate_gather(at, j):
-        block = params.at[last, at * B + column_from(j)]
-        return pltpu.make_async_remote_copy(
-            src_ref=block, dst_ref=block, send_sem=xg_s.at[j - 1], recv_sem=xg_r.at[j - 1],
-            device_id=at_dp(mate * B + b), device_id_type=MESH,
-        )
+    def x_up(j):
+        block = params.at[last, column_from(j)]
+        return pltpu.make_async_remote_copy(
+            src_ref=block, dst_ref=block, send_sem=xup_s.at[j - 1], recv_sem=xup_r.at[j - 1],
+            device_id=at_dp(jnp.minimum(me + B, n - 1)), device_id_type=MESH,
+        )
+
+    def x_down(j):
+        block = params.at[last, (A - 1) * B + column_from(j)]
+        return pltpu.make_async_remote_copy(
+            src_ref=block, dst_ref=block, send_sem=xdn_s.at[j - 1], recv_sem=xdn_r.at[j - 1],
+            device_id=at_dp(jnp.maximum(me - B, 0)), device_id_type=MESH,
+        )
+
+    def unless_end(at, p, use):
+        if balanced and p == last:
+            pl.when(jnp.logical_and(at > 0, at < A - 1))(use)
+        else:
+            use()
 
     for p in range(nproj):
         v = v_key if p == 0 else v_val
@@ -351,7 +365,7 @@
                 def across():
                     for j in range(1, B):
                         in_gather(at, j, p, b).start()
-                unless_mate(at, p, across)
+                unless_end(at, p, across)
 
             @pl.when(a + d <= A - 1)
             def _():
@@ -365,33 +379,44 @@
                 def across():
                     for j in range(1, B):
                         in_gather(at, j, p, b).start()
-                unless_mate(at, p, across)
-        if balanced and d == 2:
-            @pl.when(mated)
-            def _():
-                for j in range(1, B):
-                    in_gather(a, j, last, column_from(j)).wait_recv()
-                    mate_gather(a, j).start()
+                unless_end(at, p, across)
+        if balanced:
+            for up, near, more, copy in ((True, a == d, a < A - 1, x_up), (False, A - 1 - a == d, a > 0, x_down)):
+                @pl.when(near)
+                def _():
+                    for j in range(1, B):
+                        copy(j).wait_recv()
+
+                        @pl.when(more)
+                        def _():
+                            copy(j).start()
+                if d == 1:
+                    @pl.when(a == (0 if up else A - 1))
+                    def _():
+                        for j in range(1, B):
+                            in_gather(a, j, last, column_from(j)).wait_recv()
+                            copy(j).start()
 
     def finish(at, side, d):
         for p in range(nproj):
-            def across(p=p):
+            def raw_sent(p=p):
                 for j in range(1, B):
                     raw_copy(at, j, p).wait_send()
+
+            def sent(p=p):
+                for j in range(1, B):
                     in_gather(at, j, p, b).wait_send()
 
-            def arrive(p=p):
+            def arrived(p=p):
                 for j in range(1, B):
                     in_gather(at, j, p, column_from(j)).wait_recv()
             if side == 0:
-                across()
-                if balanced and p == last:
-                    pl.when(jnp.logical_not(mated))(arrive)
-                else:
-                    arrive()
+                raw_sent()
+                sent()
             else:
-                unless_mate(at, p, across)
-                unless_mate(at, p, arrive)
+                unless_mate(at, p, raw_sent)
+                unless_end(at, p, sent)
+            unless_end(at, p, arrived)
             if side > 0:
                 up_copy(at, p).wait_send()
             elif side < 0:
@@ -411,8 +436,9 @@
         def _():
             for j in range(1, B):
                 mate_raw(j).wait_send()
-                mate_gather(a, j).wait_send()
-                mate_gather(mate, j).wait_recv()
+        for j in range(1, B):
+            pl.when(a < A - 1)(lambda j=j: x_up(j).wait_send())
+            pl.when(a > 0)(lambda j=j: x_down(j).wait_send())
     for j in range(1, n):
         stat_copy(j).wait_send()
     for j in range(1, T):
@@ -489,7 +515,8 @@
             dma((n - 1,)), dma((n - 1,)), dma((T - 1,)), dma((T - 1,)),
             dma((A, nproj)), dma((A, nproj)), dma((A, nproj)), dma((A, nproj)),
             dma((A, inner, nproj)), dma((A, inner, nproj)),
-            dma((inner,)), dma((inner,)), dma((inner,)), dma((inner,)), dma((inner,)),
+            dma((inner,)), dma((inner,)), dma((inner,)),
+            dma((inner,)), dma((inner,)), dma((inner,)), dma((inner,)),
         ],
         compiler_params=pltpu.CompilerParams(
             collective_id=0, has_side_effects=True, vmem_limit_bytes=KERNEL_LIMIT

time: 110 us -> 107 us (0.973)
  local copies, waits for them, and re-layouts: 5.96 us -> 3.78 us
    unnamed x10 -> x8, local copies, waits for them, and re-layouts: 5.96 us -> 3.78 us
where the time goes in v3:
time: 107 us
  Pallas kernels  102 us (95%)
  local copies, waits for them, and re-layouts  3.78 us (4%)
    pallas_call x1, Pallas kernels, on_device(): pl.pallas_call(functools.partial(kernel, A, B, T, rows), name='adam_mini'...  98.9 us
    unnamed x8, local copies, waits for them, and re-layouts  3.78 us
    pallas_call x1, Pallas kernels, on_device(): pl.pallas_call(writer, name='write_out', out_shape=[jax.ShapeDtypeStruct(...  3.26 us

profile of v3, /device:TPU:0, one launch (start us, length us, event | category | flops | bytes accessed | tf_op | source)
XLA Modules:
  0.0 106.6 jit_solution(14566770678644202995)
XLA Ops:
  0.6 0.0 copy-start
  0.6 1.2 %copy-done = f32[2,512,256]{2,1,0:T(8,128)S(1)} copy-done((f32[2,512,256]{2,1,0:T(8,128)S(1)}, f32[2,512,256]{2,1,0:T(8,128)}, u32[]{:S(2)}) %copy-start) | copy-done | bytes 1048600
  1.9 0.0 copy-start.1
  1.9 1.2 %copy-done.1 = f32[2,512,256]{2,1,0:T(8,128)S(1)} copy-done((f32[2,512,256]{2,1,0:T(8,128)S(1)}, f32[2,512,256]{2,1,0:T(8,128)}, u32[]{:S(2)}) %copy-start.1) | copy-done | bytes 1048600
  3.1 0.0 copy-start.2
  3.1 0.7 copy-done.2
  3.8 0.0 copy-start.3
  3.8 0.7 copy-done.3
  4.4 98.9 %adam_mini.1 = (bf16[2,8,512,256]{3,2,1,0:T(8,128)(2,1)S(1)}, f32[2,512,256]{2,1,0:T(8,128)S(1)}, f32[2,512,256]{2,1,0:T(8,128)S(1)}, f32[2,256]{1,0:T(2,128)S(1)}) custom-call(bf16[2,8,512,256]{3,2,1,0:T(8,128)(2,1)} %bitcast.5, f32[2,512,256]{2,1,0:T(8,128)S(1)} %copy-done, f32[2,512,256]{2,1,0:T(8,128)S(1)} %copy-done.1, f32[2]{0:T(128)S(1)} %copy-done.3, ...), custom_call_target="tpu_custom_call" | custom-call | tf_op jit(solution)/shard_map/adam_mini/pallas_call | solution.py:485
  103.4 3.3 %write_out.1 = (bf16[2,8,512,256]{3,2,1,0:T(8,128)(2,1)}, f32[2,512,256]{2,1,0:T(8,128)}, f32[2,512,256]{2,1,0:T(8,128)}, f32[2]{0:T(128)}, f32[1,256]{1,0:T(1,128)}) custom-call(bf16[2,8,512,256]{3,2,1,0:T(8,128)(2,1)S(1)} %get-tuple-element.14.params, f32[2,512,256]{2,1,0:T(8,128)S(1)} %get-tuple-element.15.new_master, ...), custom_call_target="tpu_custom_call" | custom-call | tf_op jit(solution)/shard_map/write_out/pallas_call | solution.py:526
Async XLA Ops:
  0.6 1.2 %copy-start = (f32[2,512,256]{2,1,0:T(8,128)S(1)}, f32[2,512,256]{2,1,0:T(8,128)}, u32[]{:S(2)}) copy-start(f32[2,512,256]{2,1,0:T(8,128)} %master.1) | copy-start | bytes 3145732
  1.9 1.2 %copy-start.1 = (f32[2,512,256]{2,1,0:T(8,128)S(1)}, f32[2,512,256]{2,1,0:T(8,128)}, u32[]{:S(2)}) copy-start(f32[2,512,256]{2,1,0:T(8,128)} %moment.1) | copy-start | bytes 3145732
  3.1 0.7 copy-start.2
  3.8 0.7 copy-start.3
